TPU v7x, 32 devices: a whole 2x2x4 slice. The times are simulated.
32 devices in a mesh: gx: 2 (over y), gy: 4 (over x, core), gz: 4 (over z).
Axes of the slice: x: 2, y: 2, z: 4, core: 2. Of those that a mesh axis runs over, the one named last changes fastest.
Arguments:
- density: float32 [32, 64, 4096], P('gx', 'gy', 'gz'), may hold values from -19 to 19
Outputs:
- potential: float32 [32, 64, 4096], P('gx', 'gy', 'gz')
- coulomb: float32 [64, 64], replicated
All inputs are finite; a program needn't handle non-finite values.
Results may differ from a plain program's by a relative error of at most 0.000057.
Values sent between devices are 32-bit elements; how exact they have to be, the bound alone decides.
No kernel may reach another device: no remote copies, remote signals or barrier semaphores. Data moves between devices by JAX's collectives and lax.ppermute only.
A program may use at most 64 MiB of HBM per device.

v0:
```python
import jax
import jax.numpy as jnp
from jax import lax
from jax.sharding import PartitionSpec as P

PAIRS = 64
LEVELS = 6
COARSE_SWEEPS = 8
OMEGA = 2.0 / 3.0


def extended_2(x, sides, width):
    for axis, dim in sides:
        size, length = (lax.axis_size(axis), x.shape[dim])
        up = [(i, (i + 1) % size) for i in range(size - 1)]
        down = [(j, i) for i, j in up]
        last = lax.slice_in_dim(x, length - width, length, axis=dim)
        initial = lax.slice_in_dim(x, 0, width, axis=dim)
        before = lax.ppermute(last, axis, up)
        after = lax.ppermute(initial, axis, down)
        x = jnp.concatenate([before, x, after], axis=dim)
    return x


def neighbours(padded):
    total = padded[2:, 1:-1, 1:-1] + padded[:-2, 1:-1, 1:-1]
    total = total + padded[1:-1, 2:, 1:-1] + padded[1:-1, :-2, 1:-1]
    return total + padded[1:-1, 1:-1, 2:] + padded[1:-1, 1:-1, :-2]


def apply_inner(padded, factor):
    return factor * (6.0 * padded[1:-1, 1:-1, 1:-1] - neighbours(padded))


def sweep_inner(padded, source, factor):
    return padded[1:-1, 1:-1, 1:-1] + OMEGA * (source - apply_inner(padded, factor)) / (
        6.0 * factor
    )


def zero_rim(current):
    return jnp.pad(current, ((1, 1), (1, 1), (1, 1), (0, 0)))


def restrict(residual):
    size_x, size_y, size_z, count = residual.shape
    grouped = residual.reshape(size_x // 2, 2, size_y // 2, 2, size_z // 2, 2, count)
    return jnp.mean(grouped, axis=(1, 3, 5))


def prolong(correction):
    return jnp.repeat(jnp.repeat(jnp.repeat(correction, 2, axis=0), 2, axis=1), 2, axis=2)


def global_cycle(source, grid_level):
    factor = 0.25 ** (grid_level - 1)
    current = OMEGA * source / (6.0 * factor)
    if grid_level == LEVELS:
        for repeat_no in range(COARSE_SWEEPS - 1):
            current = sweep_inner(zero_rim(current), source, factor)
        return current
    current = sweep_inner(zero_rim(current), source, factor)
    residual = source - apply_inner(zero_rim(current), factor)
    current = current + prolong(global_cycle(restrict(residual), grid_level + 1))
    for repeat_no in range(2):
        current = sweep_inner(zero_rim(current), source, factor)
    return current


def arrange(stacked, block_shape):
    size_x, size_y, size_z, count = block_shape
    devs_x, devs_y, devs_z = (lax.axis_size("gx"), lax.axis_size("gy"), lax.axis_size("gz"))
    grouped = stacked.reshape(devs_x, devs_y, devs_z, size_x, size_y, size_z, count)
    grouped = grouped.transpose(0, 3, 1, 4, 2, 5, 6)
    return grouped.reshape(devs_x * size_x, devs_y * size_y, devs_z * size_z, count)


def own_block(gathered, block_shape):
    size_x, size_y, size_z, count = block_shape
    starts = (
        lax.axis_index("gx") * size_x,
        lax.axis_index("gy") * size_y,
        lax.axis_index("gz") * size_z,
        jnp.int32(0),
    )
    return lax.dynamic_slice(gathered, starts, block_shape)


def edge_mask(length, where, devices):
    position = jnp.arange(length + 2, dtype=jnp.int32) - 1 + where * length
    return (position >= 0) & (position < length * devices)


def inside_mask(block_shape):
    mask_x = edge_mask(block_shape[0], lax.axis_index("gx"), lax.axis_size("gx"))
    mask_y = edge_mask(block_shape[1], lax.axis_index("gy"), lax.axis_size("gy"))
    mask_z = edge_mask(block_shape[2], lax.axis_index("gz"), lax.axis_size("gz"))
    joined = mask_x[:, None, None] & mask_y[None, :, None] & mask_z[None, None, :]
    return joined[..., None].astype(jnp.float32)


def double_sweep(current, source, factor):
    count = current.shape[3]
    extended = extended_2(
        jnp.concatenate([current, source], axis=3), (("gx", 0), ("gy", 1), ("gz", 2)), 2
    )
    source_wide = extended[1:-1, 1:-1, 1:-1, count:]
    swept = sweep_inner(extended[..., :count], source_wide, factor) * inside_mask(current.shape)
    return swept


def distributed(source, grid_level):
    factor = 0.25 ** (grid_level - 1)
    if grid_level == LEVELS - 1:
        stacked = lax.all_gather(source[None], ("gx", "gy", "gz"), axis=0, tiled=True)
        return own_block(global_cycle(arrange(stacked, source.shape), grid_level), source.shape)
    current = OMEGA * source / (6.0 * factor)
    swept = double_sweep(current, source, factor)
    residual = source - apply_inner(swept, factor)
    current = swept[1:-1, 1:-1, 1:-1]
    current = current + prolong(distributed(restrict(residual), grid_level + 1))
    current = sweep_inner(double_sweep(current, source, factor), source, factor)
    return current


def local(density):
    cells_x, cells_y, merged = density.shape
    cells_z = merged // PAIRS
    cells = density.reshape(cells_x, cells_y, cells_z, PAIRS)
    solved = distributed(cells, 1)
    partial_block = jnp.dot(
        cells.reshape(-1, PAIRS).T,
        solved.reshape(-1, PAIRS),
        precision=lax.Precision.HIGHEST,
        preferred_element_type=jnp.float32,
    )
    summed = lax.psum(partial_block, ("gx", "gy", "gz"))
    total_cells = (
        cells_x
        * cells_y
        * cells_z
        * lax.axis_size("gx")
        * lax.axis_size("gy")
        * lax.axis_size("gz")
    )
    coulomb = summed * (4.0 / total_cells)
    return (solved.reshape(cells_x, cells_y, merged), coulomb)


def solution(mesh):
    return jax.shard_map(
        local,
        mesh=mesh,
        in_specs=(P("gx", "gy", "gz"),),
        out_specs=(P("gx", "gy", "gz"), P()),
        check_vma=False,
    )
```

profile of v0, /device:TPU:14, one launch (start us, length us, event | category | flops | bytes accessed | tf_op | source)
XLA Modules:
  0.0 362.6 jit_solution(3952595412670936373)
XLA Ops:
  6.1 4.6 %collective-permute-start.1 = (f32[2,16,16,128]{3,2,1,0:T(8,128)S(1)}, f32[2,16,16,128]{3,2,1,0:T(8,128)S(1)}, u32[]{:S(2)}, u32[]{:S(2)}) collective-permute-start(f32[2,16,16,128]{3,2,1,0:T(8,128)S(1)} %get-tuple-element.10), channel_id=1, source_target_pairs={{16,0},{17,1},{18,2},{19,3},{20,4},{21,5},{22,6},{23,7},{24,8},{25... | collective-permute-start | bytes 786440 | tf_op jit(solution)/shard_map/ppermute | solution.py:20
  10.7 4.0 %collective-permute-done = f32[2,16,16,128]{3,2,1,0:T(8,128)S(1)} collective-permute-done((f32[2,16,16,128]{3,2,1,0:T(8,128)S(1)}, f32[2,16,16,128]{3,2,1,0:T(8,128)S(1)}, u32[]{:S(2)}, u32[]{:S(2)}) %collective-permute-start) | collective-permute-done | bytes 262176 | tf_op jit(solution)/shard_map/ppermute | solution.py:19
  20.1 3.6 %collective-permute-start.3 = (f32[20,2,16,128]{3,2,1,0:T(8,128)S(1)}, f32[20,2,16,128]{3,2,1,0:T(8,128)S(1)}, u32[]{:S(2)}, u32[]{:S(2)}) collective-permute-start(f32[20,2,16,128]{3,2,1,0:T(8,128)S(1)} %get-tuple-element.19), channel_id=1, source_target_pairs={{4,0},{8,4},{12,8},{5,1},{9,5},{13,9},{6,2},{10,6},{14,10},{7,3},{... | collective-permute-start | bytes 983048 | tf_op jit(solution)/shard_map/ppermute | solution.py:20
  35.4 3.8 %collective-permute-done.4 = f32[20,20,2,128]{3,2,1,0:T(2,128)S(1)} collective-permute-done((f32[20,20,2,128]{3,2,1,0:T(2,128)S(1)}, f32[20,20,2,128]{3,2,1,0:T(2,128)S(1)}, u32[]{:S(2)}, u32[]{:S(2)}) %collective-permute-start.4) | collective-permute-done | bytes 409632 | tf_op jit(solution)/shard_map/ppermute | solution.py:19
  45.9 8.6 %fusion.23 = f32[18,18,18,64]{3,2,1,0:T(8,128)S(1)} fusion(f32[16,16,16,64]{3,2,1,0:T(8,128)S(1)} %reshape.351, f32[20,20,2,128]{3,2,1,0:T(2,128)S(1)} %collective-permute-done.4, f32[20,2,16,128]{3,2,1,0:T(8,128)S(1)} %collective-permute-done.3, f32[20,2,16,128]{3,2,1,0:T(8,128)S(1)} %collective-permute-done.2, ...), kind=kLoop, calls=%fused_computation.29 | loop fusion | flops 8584704 | bytes 14570272 | tf_op jit(solution)/shard_map/mul | solution.py:108
  62.2 4.5 %collective-permute-start.7 = (f32[2,8,8,128]{3,2,1,0:T(8,128)S(1)}, f32[2,8,8,128]{3,2,1,0:T(8,128)S(1)}, u32[]{:S(2)}, u32[]{:S(2)}) collective-permute-start(f32[2,8,8,128]{3,2,1,0:T(8,128)S(1)} %get-tuple-element.8), channel_id=1, source_target_pairs={{16,0},{17,1},{18,2},{19,3},{20,4},{21,5},{22,6},{23,7},{24,8},{25... | collective-permute-start | bytes 196616 | tf_op jit(solution)/shard_map/ppermute | solution.py:20
  70.7 3.6 %collective-permute-start.9 = (f32[12,2,8,128]{3,2,1,0:T(8,128)S(1)}, f32[12,2,8,128]{3,2,1,0:T(8,128)S(1)}, u32[]{:S(2)}, u32[]{:S(2)}) collective-permute-start(f32[12,2,8,128]{3,2,1,0:T(8,128)S(1)} %get-tuple-element.30), channel_id=1, source_target_pairs={{4,0},{8,4},{12,8},{5,1},{9,5},{13,9},{6,2},{10,6},{14,10},{7,3},{... | collective-permute-start | bytes 294920 | tf_op jit(solution)/shard_map/ppermute | solution.py:20
  91.2 4.7 %collective-permute-start.13 = (f32[2,4,4,128]{3,2,1,0:T(4,128)S(1)}, f32[2,4,4,128]{3,2,1,0:T(4,128)S(1)}, u32[]{:S(2)}, u32[]{:S(2)}) collective-permute-start(f32[2,4,4,128]{3,2,1,0:T(4,128)S(1)} %get-tuple-element.47), channel_id=1, source_target_pairs={{16,0},{17,1},{18,2},{19,3},{20,4},{21,5},{22,6},{23,7},{24,8},{25... | collective-permute-start | bytes 49160 | tf_op jit(solution)/shard_map/ppermute | solution.py:20
  106.5 3.9 %collective-permute-start.17 = (f32[8,8,2,128]{3,2,1,0:T(2,128)S(1)}, f32[8,8,2,128]{3,2,1,0:T(2,128)S(1)}, u32[]{:S(2)}, u32[]{:S(2)}) collective-permute-start(f32[8,8,2,128]{3,2,1,0:T(2,128)S(1)} %get-tuple-element.38), channel_id=1, source_target_pairs={{1,0},{2,1},{3,2},{5,4},{6,5},{7,6},{9,8},{10,9},{11,10},{13,12},{... | collective-permute-start | bytes 196616 | tf_op jit(solution)/shard_map/ppermute | solution.py:20
  114.4 4.5 %collective-permute-start.19 = (f32[2,2,2,128]{3,2,1,0:T(2,128)S(1)}, f32[2,2,2,128]{3,2,1,0:T(2,128)S(1)}, u32[]{:S(2)}, u32[]{:S(2)}) collective-permute-start(f32[2,2,2,128]{3,2,1,0:T(2,128)S(1)} %pad_maximum_fusion.46), channel_id=1, source_target_pairs={{16,0},{17,1},{18,2},{19,3},{20,4},{21,5},{22,6},{23,7},{24,8},{25... | collective-permute-start | bytes 12296 | tf_op jit(solution)/shard_map/ppermute | solution.py:20
  129.9 3.9 %collective-permute-start.23 = (f32[6,6,2,128]{3,2,1,0:T(2,128)}, f32[6,6,2,128]{3,2,1,0:T(2,128)}, u32[]{:S(2)}, u32[]{:S(2)}) collective-permute-start(f32[6,6,2,128]{3,2,1,0:T(2,128)} %fusion.211), channel_id=1, source_target_pairs={{1,0},{2,1},{3,2},{5,4},{6,5},{7,6},{9,8},{10,9},{11,10},{13,12},{... | collective-permute-start | bytes 110600 | tf_op jit(solution)/shard_map/ppermute | solution.py:20
  138.5 42.3 %all-reduce.11 = f32[2048]{0:T(1024)S(1)} all-reduce(f32[2048]{0:T(1024)S(1)} %multiply_dynamic-update-slice_fusion), channel_id=2, replica_groups=mesh['gx'=2,'gy'=4,'gz'=4] {'gx','gy','gz'}, use_global_device_ids=true, to_apply=%add.11 | all-reduce | flops 2048 | bytes 16384
  183.3 4.5 %collective-permute-start.25 = (f32[2,2,2,128]{3,2,1,0:T(2,128)S(1)}, f32[2,2,2,128]{3,2,1,0:T(2,128)S(1)}, u32[]{:S(2)}, u32[]{:S(2)}) collective-permute-start(f32[2,2,2,128]{3,2,1,0:T(2,128)S(1)} %pad_maximum_fusion.47), channel_id=1, source_target_pairs={{16,0},{17,1},{18,2},{19,3},{20,4},{21,5},{22,6},{23,7},{24,8},{25... | collective-permute-start | bytes 12296 | tf_op jit(solution)/shard_map/ppermute | solution.py:20
  206.4 4.5 %collective-permute-start.31 = (f32[2,4,4,128]{3,2,1,0:T(4,128)S(1)}, f32[2,4,4,128]{3,2,1,0:T(4,128)S(1)}, u32[]{:S(2)}, u32[]{:S(2)}) collective-permute-start(f32[2,4,4,128]{3,2,1,0:T(4,128)S(1)} %get-tuple-element.43), channel_id=1, source_target_pairs={{16,0},{17,1},{18,2},{19,3},{20,4},{21,5},{22,6},{23,7},{24,8},{25... | collective-permute-start | bytes 49160 | tf_op jit(solution)/shard_map/ppermute | solution.py:20
  221.7 3.9 %collective-permute-start.35 = (f32[8,8,2,128]{3,2,1,0:T(2,128)S(1)}, f32[8,8,2,128]{3,2,1,0:T(2,128)S(1)}, u32[]{:S(2)}, u32[]{:S(2)}) collective-permute-start(f32[8,8,2,128]{3,2,1,0:T(2,128)S(1)} %get-tuple-element.36), channel_id=1, source_target_pairs={{1,0},{2,1},{3,2},{5,4},{6,5},{7,6},{9,8},{10,9},{11,10},{13,12},{... | collective-permute-start | bytes 196616 | tf_op jit(solution)/shard_map/ppermute | solution.py:20
  230.5 4.5 %collective-permute-start.37 = (f32[2,8,8,128]{3,2,1,0:T(8,128)S(1)}, f32[2,8,8,128]{3,2,1,0:T(8,128)S(1)}, u32[]{:S(2)}, u32[]{:S(2)}) collective-permute-start(f32[2,8,8,128]{3,2,1,0:T(8,128)S(1)} %get-tuple-element.32), channel_id=1, source_target_pairs={{16,0},{17,1},{18,2},{19,3},{20,4},{21,5},{22,6},{23,7},{24,8},{25... | collective-permute-start | bytes 196616 | tf_op jit(solution)/shard_map/ppermute | solution.py:20
  247.1 3.9 %collective-permute-start.41 = (f32[12,12,2,128]{3,2,1,0:T(2,128)S(1)}, f32[12,12,2,128]{3,2,1,0:T(2,128)S(1)}, u32[]{:S(2)}, u32[]{:S(2)}) collective-permute-start(f32[12,12,2,128]{3,2,1,0:T(2,128)S(1)} %get-tuple-element.23), channel_id=1, source_target_pairs={{1,0},{2,1},{3,2},{5,4},{6,5},{7,6},{9,8},{10,9},{11,10},{13,12},{... | collective-permute-start | bytes 442376 | tf_op jit(solution)/shard_map/ppermute | solution.py:20
  260.1 4.6 %collective-permute-start.43 = (f32[2,16,16,128]{3,2,1,0:T(8,128)S(1)}, f32[2,16,16,128]{3,2,1,0:T(8,128)S(1)}, u32[]{:S(2)}, u32[]{:S(2)}) collective-permute-start(f32[2,16,16,128]{3,2,1,0:T(8,128)S(1)} %get-tuple-element.21), channel_id=1, source_target_pairs={{16,0},{17,1},{18,2},{19,3},{20,4},{21,5},{22,6},{23,7},{24,8},{25... | collective-permute-start | bytes 786440 | tf_op jit(solution)/shard_map/ppermute | solution.py:20
  271.2 3.6 %collective-permute-start.45 = (f32[20,2,16,128]{3,2,1,0:T(8,128)S(1)}, f32[20,2,16,128]{3,2,1,0:T(8,128)S(1)}, u32[]{:S(2)}, u32[]{:S(2)}) collective-permute-start(f32[20,2,16,128]{3,2,1,0:T(8,128)S(1)} %get-tuple-element.17), channel_id=1, source_target_pairs={{4,0},{8,4},{12,8},{5,1},{9,5},{13,9},{6,2},{10,6},{14,10},{7,3},{... | collective-permute-start | bytes 983048 | tf_op jit(solution)/shard_map/ppermute | solution.py:20
  283.2 4.9 %collective-permute-start.47 = (f32[20,20,2,128]{3,2,1,0:T(2,128)}, f32[20,20,2,128]{3,2,1,0:T(2,128)}, u32[]{:S(2)}, u32[]{:S(2)}) collective-permute-start(f32[20,20,2,128]{3,2,1,0:T(2,128)} %get-tuple-element.12), channel_id=1, source_target_pairs={{1,0},{2,1},{3,2},{5,4},{6,5},{7,6},{9,8},{10,9},{11,10},{13,12},{... | collective-permute-start | bytes 1228808 | tf_op jit(solution)/shard_map/ppermute | solution.py:20
  293.6 4.6 %fusion.11 = f32[20,20,20,128]{3,2,1,0:T(8,128)S(1)} fusion(f32[16,16,16,64]{3,2,1,0:T(8,128)S(1)} %reshape.351, f32[20,20,2,128]{3,2,1,0:T(2,128)} %collective-permute-done.47, f32[20,2,16,128]{3,2,1,0:T(8,128)S(1)} %collective-permute-done.45, f32[2,16,16,128]{3,2,1,0:T(8,128)S(1)} %collective-permute-done.43, f32[16,16,16,64]{3,2,1,0:T(8,128)} %copy-done.4, ...), kind=kLoop, calls=%fused_computation.13 | loop fusion | flops 7168000 | bytes 8192000 | tf_op jit(solution)/shard_map/concatenate | solution.py:21
  298.2 9.5 %fusion.35 = f32[18,18,18,64]{3,2,1,0:T(8,128)S(1)} fusion(f32[16,16,16,64]{3,2,1,0:T(8,128)S(1)} %reshape.351, f32[20,20,2,128]{3,2,1,0:T(2,128)} %collective-permute-done.46, f32[20,2,16,128]{3,2,1,0:T(8,128)S(1)} %collective-permute-done.45, f32[20,2,16,128]{3,2,1,0:T(8,128)S(1)} %collective-permute-done.44, ...), kind=kLoop, calls=%fused_computation.41 | loop fusion | flops 8584704 | bytes 14570272 | tf_op jit(solution)/shard_map/mul | solution.py:108
  313.7 5.2 %convolution_bitcast_fusion = f32[64,64]{0,1:T(8,128)S(1)} fusion(f32[4096,64]{1,0:T(8,128)S(1)} %bitcast.73, f32[4096,64]{1,0:T(8,128)} %reshape_reshape.3), kind=kOutput, calls=%fused_computation.108 | convolution fusion | flops 201326592 | bytes 2113536 | tf_op jit(solution)/shard_map/dot_general | solution.py:131
  318.9 43.0 %psum.7 = f32[64,64]{0,1:T(8,128)S(1)} all-reduce(f32[64,64]{0,1:T(8,128)S(1)} %convolution_bitcast_fusion), channel_id=1, replica_groups=mesh['gx'=2,'gy'=4,'gz'=4] {'gx','gy','gz'}, use_global_device_ids=true, to_apply=%region_6.7 | all-reduce | flops 4096 | bytes 32768 | tf_op jit(solution)/shard_map/psum | solution.py:137
  (235 shorter events, 171.8 us)
Async XLA Ops:
  4.8 9.9 %collective-permute-start = (f32[2,16,16,128]{3,2,1,0:T(8,128)S(1)}, f32[2,16,16,128]{3,2,1,0:T(8,128)S(1)}, u32[]{:S(2)}, u32[]{:S(2)}) collective-permute-start(f32[2,16,16,128]{3,2,1,0:T(8,128)S(1)} %get-tuple-element.22), channel_id=1, source_target_pairs={{0,16},{1,17},{2,18},{3,19},{4,20},{5,21},{6,22},{7,23},{8,24},{9,... | collective-permute-start | bytes 786440 | tf_op jit(solution)/shard_map/ppermute | solution.py:19
  6.1 9.8 %collective-permute-start.1 = (f32[2,16,16,128]{3,2,1,0:T(8,128)S(1)}, f32[2,16,16,128]{3,2,1,0:T(8,128)S(1)}, u32[]{:S(2)}, u32[]{:S(2)}) collective-permute-start(f32[2,16,16,128]{3,2,1,0:T(8,128)S(1)} %get-tuple-element.10), channel_id=1, source_target_pairs={{16,0},{17,1},{18,2},{19,3},{20,4},{21,5},{22,6},{23,7},{24,8},{25... | collective-permute-start | bytes 786440 | tf_op jit(solution)/shard_map/ppermute | solution.py:20
  18.2 8.4 %collective-permute-start.2 = (f32[20,2,16,128]{3,2,1,0:T(8,128)S(1)}, f32[20,2,16,128]{3,2,1,0:T(8,128)S(1)}, u32[]{:S(2)}, u32[]{:S(2)}) collective-permute-start(f32[20,2,16,128]{3,2,1,0:T(8,128)S(1)} %get-tuple-element.18), channel_id=1, source_target_pairs={{0,4},{4,8},{8,12},{1,5},{5,9},{9,13},{2,6},{6,10},{10,14},{3,7},{... | collective-permute-start | bytes 983048 | tf_op jit(solution)/shard_map/ppermute | solution.py:19
  20.1 8.2 %collective-permute-start.3 = (f32[20,2,16,128]{3,2,1,0:T(8,128)S(1)}, f32[20,2,16,128]{3,2,1,0:T(8,128)S(1)}, u32[]{:S(2)}, u32[]{:S(2)}) collective-permute-start(f32[20,2,16,128]{3,2,1,0:T(8,128)S(1)} %get-tuple-element.19), channel_id=1, source_target_pairs={{4,0},{8,4},{12,8},{5,1},{9,5},{13,9},{6,2},{10,6},{14,10},{7,3},{... | collective-permute-start | bytes 983048 | tf_op jit(solution)/shard_map/ppermute | solution.py:20
  29.3 9.8 %collective-permute-start.4 = (f32[20,20,2,128]{3,2,1,0:T(2,128)S(1)}, f32[20,20,2,128]{3,2,1,0:T(2,128)S(1)}, u32[]{:S(2)}, u32[]{:S(2)}) collective-permute-start(f32[20,20,2,128]{3,2,1,0:T(2,128)S(1)} %get-tuple-element.15), channel_id=1, source_target_pairs={{0,1},{1,2},{2,3},{4,5},{5,6},{6,7},{8,9},{9,10},{10,11},{12,13},{... | collective-permute-start | bytes 1228808 | tf_op jit(solution)/shard_map/ppermute | solution.py:19
  32.8 9.8 %collective-permute-start.5 = (f32[20,20,2,128]{3,2,1,0:T(2,128)S(1)}, f32[20,20,2,128]{3,2,1,0:T(2,128)S(1)}, u32[]{:S(2)}, u32[]{:S(2)}) collective-permute-start(f32[20,20,2,128]{3,2,1,0:T(2,128)S(1)} %get-tuple-element.14), channel_id=1, source_target_pairs={{1,0},{2,1},{3,2},{5,4},{6,5},{7,6},{9,8},{10,9},{11,10},{13,12},{... | collective-permute-start | bytes 1228808 | tf_op jit(solution)/shard_map/ppermute | solution.py:20
  60.9 6.6 %collective-permute-start.6 = (f32[2,8,8,128]{3,2,1,0:T(8,128)S(1)}, f32[2,8,8,128]{3,2,1,0:T(8,128)S(1)}, u32[]{:S(2)}, u32[]{:S(2)}) collective-permute-start(f32[2,8,8,128]{3,2,1,0:T(8,128)S(1)} %get-tuple-element.33), channel_id=1, source_target_pairs={{0,16},{1,17},{2,18},{3,19},{4,20},{5,21},{6,22},{7,23},{8,24},{9,... | collective-permute-start | bytes 196616 | tf_op jit(solution)/shard_map/ppermute | solution.py:19
  62.2 6.4 %collective-permute-start.7 = (f32[2,8,8,128]{3,2,1,0:T(8,128)S(1)}, f32[2,8,8,128]{3,2,1,0:T(8,128)S(1)}, u32[]{:S(2)}, u32[]{:S(2)}) collective-permute-start(f32[2,8,8,128]{3,2,1,0:T(8,128)S(1)} %get-tuple-element.8), channel_id=1, source_target_pairs={{16,0},{17,1},{18,2},{19,3},{20,4},{21,5},{22,6},{23,7},{24,8},{25... | collective-permute-start | bytes 196616 | tf_op jit(solution)/shard_map/ppermute | solution.py:20
  76.8 7.0 %collective-permute-start.10 = (f32[12,12,2,128]{3,2,1,0:T(2,128)S(1)}, f32[12,12,2,128]{3,2,1,0:T(2,128)S(1)}, u32[]{:S(2)}, u32[]{:S(2)}) collective-permute-start(f32[12,12,2,128]{3,2,1,0:T(2,128)S(1)} %get-tuple-element.26), channel_id=1, source_target_pairs={{0,1},{1,2},{2,3},{4,5},{5,6},{6,7},{8,9},{9,10},{10,11},{12,13},{... | collective-permute-start | bytes 442376 | tf_op jit(solution)/shard_map/ppermute | solution.py:19
  80.3 7.0 %collective-permute-start.11 = (f32[12,12,2,128]{3,2,1,0:T(2,128)S(1)}, f32[12,12,2,128]{3,2,1,0:T(2,128)S(1)}, u32[]{:S(2)}, u32[]{:S(2)}) collective-permute-start(f32[12,12,2,128]{3,2,1,0:T(2,128)S(1)} %get-tuple-element.25), channel_id=1, source_target_pairs={{1,0},{2,1},{3,2},{5,4},{6,5},{7,6},{9,8},{10,9},{11,10},{13,12},{... | collective-permute-start | bytes 442376 | tf_op jit(solution)/shard_map/ppermute | solution.py:20
  104.6 6.4 %collective-permute-start.16 = (f32[8,8,2,128]{3,2,1,0:T(2,128)S(1)}, f32[8,8,2,128]{3,2,1,0:T(2,128)S(1)}, u32[]{:S(2)}, u32[]{:S(2)}) collective-permute-start(f32[8,8,2,128]{3,2,1,0:T(2,128)S(1)} %get-tuple-element.39), channel_id=1, source_target_pairs={{0,1},{1,2},{2,3},{4,5},{5,6},{6,7},{8,9},{9,10},{10,11},{12,13},{... | collective-permute-start | bytes 196616 | tf_op jit(solution)/shard_map/ppermute | solution.py:19
  106.5 6.2 %collective-permute-start.17 = (f32[8,8,2,128]{3,2,1,0:T(2,128)S(1)}, f32[8,8,2,128]{3,2,1,0:T(2,128)S(1)}, u32[]{:S(2)}, u32[]{:S(2)}) collective-permute-start(f32[8,8,2,128]{3,2,1,0:T(2,128)S(1)} %get-tuple-element.38), channel_id=1, source_target_pairs={{1,0},{2,1},{3,2},{5,4},{6,5},{7,6},{9,8},{10,9},{11,10},{13,12},{... | collective-permute-start | bytes 196616 | tf_op jit(solution)/shard_map/ppermute | solution.py:20
  113.1 6.6 %collective-permute-start.18 = (f32[2,2,2,128]{3,2,1,0:T(2,128)S(1)}, f32[2,2,2,128]{3,2,1,0:T(2,128)S(1)}, u32[]{:S(2)}, u32[]{:S(2)}) collective-permute-start(f32[2,2,2,128]{3,2,1,0:T(2,128)S(1)} %pad_maximum_fusion.46), channel_id=1, source_target_pairs={{0,16},{1,17},{2,18},{3,19},{4,20},{5,21},{6,22},{7,23},{8,24},{9,... | collective-permute-start | bytes 12296 | tf_op jit(solution)/shard_map/ppermute | solution.py:19
  129.9 6.2 %collective-permute-start.23 = (f32[6,6,2,128]{3,2,1,0:T(2,128)}, f32[6,6,2,128]{3,2,1,0:T(2,128)}, u32[]{:S(2)}, u32[]{:S(2)}) collective-permute-start(f32[6,6,2,128]{3,2,1,0:T(2,128)} %fusion.211), channel_id=1, source_target_pairs={{1,0},{2,1},{3,2},{5,4},{6,5},{7,6},{9,8},{10,9},{11,10},{13,12},{... | collective-permute-start | bytes 110600 | tf_op jit(solution)/shard_map/ppermute | solution.py:20
  219.8 6.2 %collective-permute-start.34 = (f32[8,8,2,128]{3,2,1,0:T(2,128)S(1)}, f32[8,8,2,128]{3,2,1,0:T(2,128)S(1)}, u32[]{:S(2)}, u32[]{:S(2)}) collective-permute-start(f32[8,8,2,128]{3,2,1,0:T(2,128)S(1)} %get-tuple-element.37), channel_id=1, source_target_pairs={{0,1},{1,2},{2,3},{4,5},{5,6},{6,7},{8,9},{9,10},{10,11},{12,13},{... | collective-permute-start | bytes 196616 | tf_op jit(solution)/shard_map/ppermute | solution.py:19
  230.5 6.4 %collective-permute-start.37 = (f32[2,8,8,128]{3,2,1,0:T(8,128)S(1)}, f32[2,8,8,128]{3,2,1,0:T(8,128)S(1)}, u32[]{:S(2)}, u32[]{:S(2)}) collective-permute-start(f32[2,8,8,128]{3,2,1,0:T(8,128)S(1)} %get-tuple-element.32), channel_id=1, source_target_pairs={{16,0},{17,1},{18,2},{19,3},{20,4},{21,5},{22,6},{23,7},{24,8},{25... | collective-permute-start | bytes 196616 | tf_op jit(solution)/shard_map/ppermute | solution.py:20
  245.2 7.0 %collective-permute-start.40 = (f32[12,12,2,128]{3,2,1,0:T(2,128)S(1)}, f32[12,12,2,128]{3,2,1,0:T(2,128)S(1)}, u32[]{:S(2)}, u32[]{:S(2)}) collective-permute-start(f32[12,12,2,128]{3,2,1,0:T(2,128)S(1)} %get-tuple-element.24), channel_id=1, source_target_pairs={{0,1},{1,2},{2,3},{4,5},{5,6},{6,7},{8,9},{9,10},{10,11},{12,13},{... | collective-permute-start | bytes 442376 | tf_op jit(solution)/shard_map/ppermute | solution.py:19
  247.1 7.0 %collective-permute-start.41 = (f32[12,12,2,128]{3,2,1,0:T(2,128)S(1)}, f32[12,12,2,128]{3,2,1,0:T(2,128)S(1)}, u32[]{:S(2)}, u32[]{:S(2)}) collective-permute-start(f32[12,12,2,128]{3,2,1,0:T(2,128)S(1)} %get-tuple-element.23), channel_id=1, source_target_pairs={{1,0},{2,1},{3,2},{5,4},{6,5},{7,6},{9,8},{10,9},{11,10},{13,12},{... | collective-permute-start | bytes 442376 | tf_op jit(solution)/shard_map/ppermute | solution.py:20
  258.8 8.3 %collective-permute-start.42 = (f32[2,16,16,128]{3,2,1,0:T(8,128)S(1)}, f32[2,16,16,128]{3,2,1,0:T(8,128)S(1)}, u32[]{:S(2)}, u32[]{:S(2)}) collective-permute-start(f32[2,16,16,128]{3,2,1,0:T(8,128)S(1)} %get-tuple-element.20), channel_id=1, source_target_pairs={{0,16},{1,17},{2,18},{3,19},{4,20},{5,21},{6,22},{7,23},{8,24},{9,... | collective-permute-start | bytes 786440 | tf_op jit(solution)/shard_map/ppermute | solution.py:19
  260.1 8.4 %collective-permute-start.43 = (f32[2,16,16,128]{3,2,1,0:T(8,128)S(1)}, f32[2,16,16,128]{3,2,1,0:T(8,128)S(1)}, u32[]{:S(2)}, u32[]{:S(2)}) collective-permute-start(f32[2,16,16,128]{3,2,1,0:T(8,128)S(1)} %get-tuple-element.21), channel_id=1, source_target_pairs={{16,0},{17,1},{18,2},{19,3},{20,4},{21,5},{22,6},{23,7},{24,8},{25... | collective-permute-start | bytes 786440 | tf_op jit(solution)/shard_map/ppermute | solution.py:20
  269.3 8.4 %collective-permute-start.44 = (f32[20,2,16,128]{3,2,1,0:T(8,128)S(1)}, f32[20,2,16,128]{3,2,1,0:T(8,128)S(1)}, u32[]{:S(2)}, u32[]{:S(2)}) collective-permute-start(f32[20,2,16,128]{3,2,1,0:T(8,128)S(1)} %get-tuple-element.16), channel_id=1, source_target_pairs={{0,4},{4,8},{8,12},{1,5},{5,9},{9,13},{2,6},{6,10},{10,14},{3,7},{... | collective-permute-start | bytes 983048 | tf_op jit(solution)/shard_map/ppermute | solution.py:19
  271.2 8.2 %collective-permute-start.45 = (f32[20,2,16,128]{3,2,1,0:T(8,128)S(1)}, f32[20,2,16,128]{3,2,1,0:T(8,128)S(1)}, u32[]{:S(2)}, u32[]{:S(2)}) collective-permute-start(f32[20,2,16,128]{3,2,1,0:T(8,128)S(1)} %get-tuple-element.17), channel_id=1, source_target_pairs={{4,0},{8,4},{12,8},{5,1},{9,5},{13,9},{6,2},{10,6},{14,10},{7,3},{... | collective-permute-start | bytes 983048 | tf_op jit(solution)/shard_map/ppermute | solution.py:20
  281.3 10.2 %collective-permute-start.46 = (f32[20,20,2,128]{3,2,1,0:T(2,128)}, f32[20,20,2,128]{3,2,1,0:T(2,128)}, u32[]{:S(2)}, u32[]{:S(2)}) collective-permute-start(f32[20,20,2,128]{3,2,1,0:T(2,128)} %get-tuple-element.13), channel_id=1, source_target_pairs={{0,1},{1,2},{2,3},{4,5},{5,6},{6,7},{8,9},{9,10},{10,11},{12,13},{... | collective-permute-start | bytes 1228808 | tf_op jit(solution)/shard_map/ppermute | solution.py:19
  283.2 10.5 %collective-permute-start.47 = (f32[20,20,2,128]{3,2,1,0:T(2,128)}, f32[20,20,2,128]{3,2,1,0:T(2,128)}, u32[]{:S(2)}, u32[]{:S(2)}) collective-permute-start(f32[20,20,2,128]{3,2,1,0:T(2,128)} %get-tuple-element.12), channel_id=1, source_target_pairs={{1,0},{2,1},{3,2},{5,4},{6,5},{7,6},{9,8},{10,9},{11,10},{13,12},{... | collective-permute-start | bytes 1228808 | tf_op jit(solution)/shard_map/ppermute | solution.py:20
  (43 other events, 433.5 us)
where the time goes:
time: 365 us; the launch traced here: 363 us
  starting transfers between devices  139 us (38%)
  blocking collectives  85.3 us (23%)
  waiting for transfers between devices  62.1 us (17%)
  other arithmetic  54.9 us (15%)
  local copies, waits for them, and re-layouts  14.3 us (4%)
  matrix products  5.15 us (1%)
    ppermute x24, starting transfers between devices, extended_2(): after = lax.ppermute(initial, axis, down)  94.3 us
    ppermute x24, starting transfers between devices, extended_2(): before = lax.ppermute(last, axis, up)  44.7 us
    psum x1, blocking collectives, local(): summed = lax.psum(partial_block, ('gx', 'gy', 'gz'))  43 us
    unnamed x1, blocking collectives  42.3 us
    ppermute x24, waiting for transfers between devices, extended_2(): after = lax.ppermute(initial, axis, down)  42.2 us
    mul x8, other arithmetic, double_sweep(): sweep_inner(extended[..., :count], source_wide, factor)  23.4 us
    ppermute x24, waiting for transfers between devices, extended_2(): before = lax.ppermute(last, axis, up)  19.9 us
    concatenate x24, other arithmetic, extended_2(): x = jnp.concatenate([before, x, after], axis=dim)  15.6 us
  transfers between devices with their start and end apart: 48, of which 37 were waited for; matrix products, arithmetic and copies ran while one was open for 1% of the time, Pallas kernels for 0%

commit v1 on v0

--- a/solution.py
+++ b/solution.py
@@ -134,7 +134,7 @@
         precision=lax.Precision.HIGHEST,
         preferred_element_type=jnp.float32,
     )
-    summed = lax.psum(partial_block, ("gx", "gy", "gz"))
+    summed = lax.psum(lax.psum(partial_block, ("gy", "gz")), "gx")
     total_cells = (
         cells_x
         * cells_y

time: 365 us -> 391 us (1.071)
  blocking collectives: 85.3 us -> 110 us
    psum x1 -> x2, blocking collectives: 43 us -> 68 us  [local(): summed = lax.psum(lax.psum(partial_block, ('gy', 'gz')), 'gx')]
where the time goes in v1:
time: 391 us; the launch traced here: 388 us
  starting transfers between devices  139 us (36%)
  blocking collectives  110 us (28%)
  waiting for transfers between devices  62.1 us (16%)
  other arithmetic  54.9 us (14%)
  local copies, waits for them, and re-layouts  14.3 us (4%)
  matrix products  5.15 us (1%)
    ppermute x24, starting transfers between devices, extended_2(): after = lax.ppermute(initial, axis, down)  94.3 us
    psum x2, blocking collectives, local(): summed = lax.psum(lax.psum(partial_block, ('gy', 'gz')), 'gx')  68 us
    ppermute x24, starting transfers between devices, extended_2(): before = lax.ppermute(last, axis, up)  44.7 us
    unnamed x1, blocking collectives  42.3 us
    ppermute x24, waiting for transfers between devices, extended_2(): after = lax.ppermute(initial, axis, down)  42.2 us
    mul x8, other arithmetic, double_sweep(): sweep_inner(extended[..., :count], source_wide, factor)  23.4 us
    ppermute x24, waiting for transfers between devices, extended_2(): before = lax.ppermute(last, axis, up)  19.9 us
    concatenate x24, other arithmetic, extended_2(): x = jnp.concatenate([before, x, after], axis=dim)  15.6 us
  transfers between devices with their start and end apart: 48, of which 37 were waited for; matrix products, arithmetic and copies ran while one was open for 1% of the time, Pallas kernels for 0%

profile of v1, /device:TPU:14, one launch (start us, length us, event | category | flops | bytes accessed | tf_op | source)
XLA Modules:
  0.0 387.6 jit_solution(13496438437662713241)
XLA Ops:
  6.1 4.6 %collective-permute-start.1 = (f32[2,16,16,128]{3,2,1,0:T(8,128)S(1)}, f32[2,16,16,128]{3,2,1,0:T(8,128)S(1)}, u32[]{:S(2)}, u32[]{:S(2)}) collective-permute-start(f32[2,16,16,128]{3,2,1,0:T(8,128)S(1)} %get-tuple-element.10), channel_id=1, source_target_pairs={{16,0},{17,1},{18,2},{19,3},{20,4},{21,5},{22,6},{23,7},{24,8},{25... | collective-permute-start | bytes 786440 | tf_op jit(solution)/shard_map/ppermute | solution.py:20
  10.7 4.0 %collective-permute-done = f32[2,16,16,128]{3,2,1,0:T(8,128)S(1)} collective-permute-done((f32[2,16,16,128]{3,2,1,0:T(8,128)S(1)}, f32[2,16,16,128]{3,2,1,0:T(8,128)S(1)}, u32[]{:S(2)}, u32[]{:S(2)}) %collective-permute-start) | collective-permute-done | bytes 262176 | tf_op jit(solution)/shard_map/ppermute | solution.py:19
  20.1 3.6 collective-permute-start.3
  35.4 3.8 collective-permute-done.4
  45.9 8.6 %fusion.23 = f32[18,18,18,64]{3,2,1,0:T(8,128)S(1)} fusion(f32[16,16,16,64]{3,2,1,0:T(8,128)S(1)} %reshape.351, f32[20,20,2,128]{3,2,1,0:T(2,128)S(1)} %collective-permute-done.4, f32[20,2,16,128]{3,2,1,0:T(8,128)S(1)} %collective-permute-done.3, f32[20,2,16,128]{3,2,1,0:T(8,128)S(1)} %collective-permute-done.2, ...), kind=kLoop, calls=%fused_computation.29 | loop fusion | flops 8584704 | bytes 14570272 | tf_op jit(solution)/shard_map/mul | solution.py:108
  62.2 4.5 %collective-permute-start.7 = (f32[2,8,8,128]{3,2,1,0:T(8,128)S(1)}, f32[2,8,8,128]{3,2,1,0:T(8,128)S(1)}, u32[]{:S(2)}, u32[]{:S(2)}) collective-permute-start(f32[2,8,8,128]{3,2,1,0:T(8,128)S(1)} %get-tuple-element.8), channel_id=1, source_target_pairs={{16,0},{17,1},{18,2},{19,3},{20,4},{21,5},{22,6},{23,7},{24,8},{25... | collective-permute-start | bytes 196616 | tf_op jit(solution)/shard_map/ppermute | solution.py:20
  70.7 3.6 collective-permute-start.9
  91.2 4.7 %collective-permute-start.13 = (f32[2,4,4,128]{3,2,1,0:T(4,128)S(1)}, f32[2,4,4,128]{3,2,1,0:T(4,128)S(1)}, u32[]{:S(2)}, u32[]{:S(2)}) collective-permute-start(f32[2,4,4,128]{3,2,1,0:T(4,128)S(1)} %get-tuple-element.47), channel_id=1, source_target_pairs={{16,0},{17,1},{18,2},{19,3},{20,4},{21,5},{22,6},{23,7},{24,8},{25... | collective-permute-start | bytes 49160 | tf_op jit(solution)/shard_map/ppermute | solution.py:20
  106.5 3.9 %collective-permute-start.17 = (f32[8,8,2,128]{3,2,1,0:T(2,128)S(1)}, f32[8,8,2,128]{3,2,1,0:T(2,128)S(1)}, u32[]{:S(2)}, u32[]{:S(2)}) collective-permute-start(f32[8,8,2,128]{3,2,1,0:T(2,128)S(1)} %get-tuple-element.38), channel_id=1, source_target_pairs={{1,0},{2,1},{3,2},{5,4},{6,5},{7,6},{9,8},{10,9},{11,10},{13,12},{... | collective-permute-start | bytes 196616 | tf_op jit(solution)/shard_map/ppermute | solution.py:20
  114.4 4.5 %collective-permute-start.19 = (f32[2,2,2,128]{3,2,1,0:T(2,128)S(1)}, f32[2,2,2,128]{3,2,1,0:T(2,128)S(1)}, u32[]{:S(2)}, u32[]{:S(2)}) collective-permute-start(f32[2,2,2,128]{3,2,1,0:T(2,128)S(1)} %pad_maximum_fusion.46), channel_id=1, source_target_pairs={{16,0},{17,1},{18,2},{19,3},{20,4},{21,5},{22,6},{23,7},{24,8},{25... | collective-permute-start | bytes 12296 | tf_op jit(solution)/shard_map/ppermute | solution.py:20
  129.9 3.9 %collective-permute-start.23 = (f32[6,6,2,128]{3,2,1,0:T(2,128)}, f32[6,6,2,128]{3,2,1,0:T(2,128)}, u32[]{:S(2)}, u32[]{:S(2)}) collective-permute-start(f32[6,6,2,128]{3,2,1,0:T(2,128)} %fusion.211), channel_id=1, source_target_pairs={{1,0},{2,1},{3,2},{5,4},{6,5},{7,6},{9,8},{10,9},{11,10},{13,12},{... | collective-permute-start | bytes 110600 | tf_op jit(solution)/shard_map/ppermute | solution.py:20
  138.5 42.3 %all-reduce.11 = f32[2048]{0:T(1024)S(1)} all-reduce(f32[2048]{0:T(1024)S(1)} %multiply_dynamic-update-slice_fusion), channel_id=2, replica_groups=mesh['gx'=2,'gy'=4,'gz'=4] {'gx','gy','gz'}, use_global_device_ids=true, to_apply=%add.11 | all-reduce | flops 2048 | bytes 16384
  183.3 4.5 %collective-permute-start.25 = (f32[2,2,2,128]{3,2,1,0:T(2,128)S(1)}, f32[2,2,2,128]{3,2,1,0:T(2,128)S(1)}, u32[]{:S(2)}, u32[]{:S(2)}) collective-permute-start(f32[2,2,2,128]{3,2,1,0:T(2,128)S(1)} %pad_maximum_fusion.47), channel_id=1, source_target_pairs={{16,0},{17,1},{18,2},{19,3},{20,4},{21,5},{22,6},{23,7},{24,8},{25... | collective-permute-start | bytes 12296 | tf_op jit(solution)/shard_map/ppermute | solution.py:20
  206.4 4.5 %collective-permute-start.31 = (f32[2,4,4,128]{3,2,1,0:T(4,128)S(1)}, f32[2,4,4,128]{3,2,1,0:T(4,128)S(1)}, u32[]{:S(2)}, u32[]{:S(2)}) collective-permute-start(f32[2,4,4,128]{3,2,1,0:T(4,128)S(1)} %get-tuple-element.43), channel_id=1, source_target_pairs={{16,0},{17,1},{18,2},{19,3},{20,4},{21,5},{22,6},{23,7},{24,8},{25... | collective-permute-start | bytes 49160 | tf_op jit(solution)/shard_map/ppermute | solution.py:20
  221.7 3.9 %collective-permute-start.35 = (f32[8,8,2,128]{3,2,1,0:T(2,128)S(1)}, f32[8,8,2,128]{3,2,1,0:T(2,128)S(1)}, u32[]{:S(2)}, u32[]{:S(2)}) collective-permute-start(f32[8,8,2,128]{3,2,1,0:T(2,128)S(1)} %get-tuple-element.36), channel_id=1, source_target_pairs={{1,0},{2,1},{3,2},{5,4},{6,5},{7,6},{9,8},{10,9},{11,10},{13,12},{... | collective-permute-start | bytes 196616 | tf_op jit(solution)/shard_map/ppermute | solution.py:20
  230.5 4.5 %collective-permute-start.37 = (f32[2,8,8,128]{3,2,1,0:T(8,128)S(1)}, f32[2,8,8,128]{3,2,1,0:T(8,128)S(1)}, u32[]{:S(2)}, u32[]{:S(2)}) collective-permute-start(f32[2,8,8,128]{3,2,1,0:T(8,128)S(1)} %get-tuple-element.32), channel_id=1, source_target_pairs={{16,0},{17,1},{18,2},{19,3},{20,4},{21,5},{22,6},{23,7},{24,8},{25... | collective-permute-start | bytes 196616 | tf_op jit(solution)/shard_map/ppermute | solution.py:20
  247.1 3.9 %collective-permute-start.41 = (f32[12,12,2,128]{3,2,1,0:T(2,128)S(1)}, f32[12,12,2,128]{3,2,1,0:T(2,128)S(1)}, u32[]{:S(2)}, u32[]{:S(2)}) collective-permute-start(f32[12,12,2,128]{3,2,1,0:T(2,128)S(1)} %get-tuple-element.23), channel_id=1, source_target_pairs={{1,0},{2,1},{3,2},{5,4},{6,5},{7,6},{9,8},{10,9},{11,10},{13,12},{... | collective-permute-start | bytes 442376 | tf_op jit(solution)/shard_map/ppermute | solution.py:20
  260.1 4.6 %collective-permute-start.43 = (f32[2,16,16,128]{3,2,1,0:T(8,128)S(1)}, f32[2,16,16,128]{3,2,1,0:T(8,128)S(1)}, u32[]{:S(2)}, u32[]{:S(2)}) collective-permute-start(f32[2,16,16,128]{3,2,1,0:T(8,128)S(1)} %get-tuple-element.21), channel_id=1, source_target_pairs={{16,0},{17,1},{18,2},{19,3},{20,4},{21,5},{22,6},{23,7},{24,8},{25... | collective-permute-start | bytes 786440 | tf_op jit(solution)/shard_map/ppermute | solution.py:20
  283.2 4.9 %collective-permute-start.47 = (f32[20,20,2,128]{3,2,1,0:T(2,128)}, f32[20,20,2,128]{3,2,1,0:T(2,128)}, u32[]{:S(2)}, u32[]{:S(2)}) collective-permute-start(f32[20,20,2,128]{3,2,1,0:T(2,128)} %get-tuple-element.12), channel_id=1, source_target_pairs={{1,0},{2,1},{3,2},{5,4},{6,5},{7,6},{9,8},{10,9},{11,10},{13,12},{... | collective-permute-start | bytes 1228808 | tf_op jit(solution)/shard_map/ppermute | solution.py:20
  293.6 4.6 %fusion.11 = f32[20,20,20,128]{3,2,1,0:T(8,128)S(1)} fusion(f32[16,16,16,64]{3,2,1,0:T(8,128)S(1)} %reshape.351, f32[20,20,2,128]{3,2,1,0:T(2,128)} %collective-permute-done.47, f32[20,2,16,128]{3,2,1,0:T(8,128)S(1)} %collective-permute-done.45, f32[2,16,16,128]{3,2,1,0:T(8,128)S(1)} %collective-permute-done.43, f32[16,16,16,64]{3,2,1,0:T(8,128)} %copy-done.4, ...), kind=kLoop, calls=%fused_computation.13 | loop fusion | flops 7168000 | bytes 8192000 | tf_op jit(solution)/shard_map/concatenate | solution.py:21
  298.2 9.5 %fusion.35 = f32[18,18,18,64]{3,2,1,0:T(8,128)S(1)} fusion(f32[16,16,16,64]{3,2,1,0:T(8,128)S(1)} %reshape.351, f32[20,20,2,128]{3,2,1,0:T(2,128)} %collective-permute-done.46, f32[20,2,16,128]{3,2,1,0:T(8,128)S(1)} %collective-permute-done.45, f32[20,2,16,128]{3,2,1,0:T(8,128)S(1)} %collective-permute-done.44, ...), kind=kLoop, calls=%fused_computation.41 | loop fusion | flops 8584704 | bytes 14570272 | tf_op jit(solution)/shard_map/mul | solution.py:108
  313.7 5.2 %convolution_bitcast_fusion = f32[64,64]{0,1:T(8,128)S(1)} fusion(f32[4096,64]{1,0:T(8,128)S(1)} %bitcast.73, f32[4096,64]{1,0:T(8,128)} %reshape_reshape.3), kind=kOutput, calls=%fused_computation.108 | convolution fusion | flops 201326592 | bytes 2113536 | tf_op jit(solution)/shard_map/dot_general | solution.py:131
  318.9 58.7 %psum.14 = f32[64,64]{0,1:T(8,128)S(1)} all-reduce(f32[64,64]{0,1:T(8,128)S(1)} %convolution_bitcast_fusion), channel_id=1, replica_groups=mesh['gx'=2,'gy'=4,'gz'=4] {'gy','gz'}, use_global_device_ids=true, to_apply=%region_6.7 | all-reduce | flops 4096 | bytes 32768 | tf_op jit(solution)/shard_map/psum | solution.py:137
  377.5 9.3 %psum.15 = f32[64,64]{0,1:T(8,128)S(1)} all-reduce(f32[64,64]{0,1:T(8,128)S(1)} %psum.14), channel_id=1, replica_groups=mesh['gx'=2,'gy'=4,'gz'=4] {'gx'}, use_global_device_ids=true, to_apply=%region_7.8 | all-reduce | flops 4096 | bytes 32768 | tf_op jit(solution)/shard_map/psum | solution.py:137
  (236 shorter events, 175.5 us)
Async XLA Ops:
  4.8 9.9 %collective-permute-start = (f32[2,16,16,128]{3,2,1,0:T(8,128)S(1)}, f32[2,16,16,128]{3,2,1,0:T(8,128)S(1)}, u32[]{:S(2)}, u32[]{:S(2)}) collective-permute-start(f32[2,16,16,128]{3,2,1,0:T(8,128)S(1)} %get-tuple-element.22), channel_id=1, source_target_pairs={{0,16},{1,17},{2,18},{3,19},{4,20},{5,21},{6,22},{7,23},{8,24},{9,... | collective-permute-start | bytes 786440 | tf_op jit(solution)/shard_map/ppermute | solution.py:19
  6.1 9.8 %collective-permute-start.1 = (f32[2,16,16,128]{3,2,1,0:T(8,128)S(1)}, f32[2,16,16,128]{3,2,1,0:T(8,128)S(1)}, u32[]{:S(2)}, u32[]{:S(2)}) collective-permute-start(f32[2,16,16,128]{3,2,1,0:T(8,128)S(1)} %get-tuple-element.10), channel_id=1, source_target_pairs={{16,0},{17,1},{18,2},{19,3},{20,4},{21,5},{22,6},{23,7},{24,8},{25... | collective-permute-start | bytes 786440 | tf_op jit(solution)/shard_map/ppermute | solution.py:20
  18.2 8.4 %collective-permute-start.2 = (f32[20,2,16,128]{3,2,1,0:T(8,128)S(1)}, f32[20,2,16,128]{3,2,1,0:T(8,128)S(1)}, u32[]{:S(2)}, u32[]{:S(2)}) collective-permute-start(f32[20,2,16,128]{3,2,1,0:T(8,128)S(1)} %get-tuple-element.18), channel_id=1, source_target_pairs={{0,4},{4,8},{8,12},{1,5},{5,9},{9,13},{2,6},{6,10},{10,14},{3,7},{... | collective-permute-start | bytes 983048 | tf_op jit(solution)/shard_map/ppermute | solution.py:19
  20.1 8.2 %collective-permute-start.3 = (f32[20,2,16,128]{3,2,1,0:T(8,128)S(1)}, f32[20,2,16,128]{3,2,1,0:T(8,128)S(1)}, u32[]{:S(2)}, u32[]{:S(2)}) collective-permute-start(f32[20,2,16,128]{3,2,1,0:T(8,128)S(1)} %get-tuple-element.19), channel_id=1, source_target_pairs={{4,0},{8,4},{12,8},{5,1},{9,5},{13,9},{6,2},{10,6},{14,10},{7,3},{... | collective-permute-start | bytes 983048 | tf_op jit(solution)/shard_map/ppermute | solution.py:20
  29.3 9.8 %collective-permute-start.4 = (f32[20,20,2,128]{3,2,1,0:T(2,128)S(1)}, f32[20,20,2,128]{3,2,1,0:T(2,128)S(1)}, u32[]{:S(2)}, u32[]{:S(2)}) collective-permute-start(f32[20,20,2,128]{3,2,1,0:T(2,128)S(1)} %get-tuple-element.15), channel_id=1, source_target_pairs={{0,1},{1,2},{2,3},{4,5},{5,6},{6,7},{8,9},{9,10},{10,11},{12,13},{... | collective-permute-start | bytes 1228808 | tf_op jit(solution)/shard_map/ppermute | solution.py:19
  32.8 9.8 %collective-permute-start.5 = (f32[20,20,2,128]{3,2,1,0:T(2,128)S(1)}, f32[20,20,2,128]{3,2,1,0:T(2,128)S(1)}, u32[]{:S(2)}, u32[]{:S(2)}) collective-permute-start(f32[20,20,2,128]{3,2,1,0:T(2,128)S(1)} %get-tuple-element.14), channel_id=1, source_target_pairs={{1,0},{2,1},{3,2},{5,4},{6,5},{7,6},{9,8},{10,9},{11,10},{13,12},{... | collective-permute-start | bytes 1228808 | tf_op jit(solution)/shard_map/ppermute | solution.py:20
  60.9 6.6 %collective-permute-start.6 = (f32[2,8,8,128]{3,2,1,0:T(8,128)S(1)}, f32[2,8,8,128]{3,2,1,0:T(8,128)S(1)}, u32[]{:S(2)}, u32[]{:S(2)}) collective-permute-start(f32[2,8,8,128]{3,2,1,0:T(8,128)S(1)} %get-tuple-element.33), channel_id=1, source_target_pairs={{0,16},{1,17},{2,18},{3,19},{4,20},{5,21},{6,22},{7,23},{8,24},{9,... | collective-permute-start | bytes 196616 | tf_op jit(solution)/shard_map/ppermute | solution.py:19
  62.2 6.4 %collective-permute-start.7 = (f32[2,8,8,128]{3,2,1,0:T(8,128)S(1)}, f32[2,8,8,128]{3,2,1,0:T(8,128)S(1)}, u32[]{:S(2)}, u32[]{:S(2)}) collective-permute-start(f32[2,8,8,128]{3,2,1,0:T(8,128)S(1)} %get-tuple-element.8), channel_id=1, source_target_pairs={{16,0},{17,1},{18,2},{19,3},{20,4},{21,5},{22,6},{23,7},{24,8},{25... | collective-permute-start | bytes 196616 | tf_op jit(solution)/shard_map/ppermute | solution.py:20
  76.8 7.0 %collective-permute-start.10 = (f32[12,12,2,128]{3,2,1,0:T(2,128)S(1)}, f32[12,12,2,128]{3,2,1,0:T(2,128)S(1)}, u32[]{:S(2)}, u32[]{:S(2)}) collective-permute-start(f32[12,12,2,128]{3,2,1,0:T(2,128)S(1)} %get-tuple-element.26), channel_id=1, source_target_pairs={{0,1},{1,2},{2,3},{4,5},{5,6},{6,7},{8,9},{9,10},{10,11},{12,13},{... | collective-permute-start | bytes 442376 | tf_op jit(solution)/shard_map/ppermute | solution.py:19
  80.3 7.0 %collective-permute-start.11 = (f32[12,12,2,128]{3,2,1,0:T(2,128)S(1)}, f32[12,12,2,128]{3,2,1,0:T(2,128)S(1)}, u32[]{:S(2)}, u32[]{:S(2)}) collective-permute-start(f32[12,12,2,128]{3,2,1,0:T(2,128)S(1)} %get-tuple-element.25), channel_id=1, source_target_pairs={{1,0},{2,1},{3,2},{5,4},{6,5},{7,6},{9,8},{10,9},{11,10},{13,12},{... | collective-permute-start | bytes 442376 | tf_op jit(solution)/shard_map/ppermute | solution.py:20
  104.6 6.4 %collective-permute-start.16 = (f32[8,8,2,128]{3,2,1,0:T(2,128)S(1)}, f32[8,8,2,128]{3,2,1,0:T(2,128)S(1)}, u32[]{:S(2)}, u32[]{:S(2)}) collective-permute-start(f32[8,8,2,128]{3,2,1,0:T(2,128)S(1)} %get-tuple-element.39), channel_id=1, source_target_pairs={{0,1},{1,2},{2,3},{4,5},{5,6},{6,7},{8,9},{9,10},{10,11},{12,13},{... | collective-permute-start | bytes 196616 | tf_op jit(solution)/shard_map/ppermute | solution.py:19
  106.5 6.2 %collective-permute-start.17 = (f32[8,8,2,128]{3,2,1,0:T(2,128)S(1)}, f32[8,8,2,128]{3,2,1,0:T(2,128)S(1)}, u32[]{:S(2)}, u32[]{:S(2)}) collective-permute-start(f32[8,8,2,128]{3,2,1,0:T(2,128)S(1)} %get-tuple-element.38), channel_id=1, source_target_pairs={{1,0},{2,1},{3,2},{5,4},{6,5},{7,6},{9,8},{10,9},{11,10},{13,12},{... | collective-permute-start | bytes 196616 | tf_op jit(solution)/shard_map/ppermute | solution.py:20
  113.1 6.6 %collective-permute-start.18 = (f32[2,2,2,128]{3,2,1,0:T(2,128)S(1)}, f32[2,2,2,128]{3,2,1,0:T(2,128)S(1)}, u32[]{:S(2)}, u32[]{:S(2)}) collective-permute-start(f32[2,2,2,128]{3,2,1,0:T(2,128)S(1)} %pad_maximum_fusion.46), channel_id=1, source_target_pairs={{0,16},{1,17},{2,18},{3,19},{4,20},{5,21},{6,22},{7,23},{8,24},{9,... | collective-permute-start | bytes 12296 | tf_op jit(solution)/shard_map/ppermute | solution.py:19
  129.9 6.2 %collective-permute-start.23 = (f32[6,6,2,128]{3,2,1,0:T(2,128)}, f32[6,6,2,128]{3,2,1,0:T(2,128)}, u32[]{:S(2)}, u32[]{:S(2)}) collective-permute-start(f32[6,6,2,128]{3,2,1,0:T(2,128)} %fusion.211), channel_id=1, source_target_pairs={{1,0},{2,1},{3,2},{5,4},{6,5},{7,6},{9,8},{10,9},{11,10},{13,12},{... | collective-permute-start | bytes 110600 | tf_op jit(solution)/shard_map/ppermute | solution.py:20
  221.7 6.2 %collective-permute-start.35 = (f32[8,8,2,128]{3,2,1,0:T(2,128)S(1)}, f32[8,8,2,128]{3,2,1,0:T(2,128)S(1)}, u32[]{:S(2)}, u32[]{:S(2)}) collective-permute-start(f32[8,8,2,128]{3,2,1,0:T(2,128)S(1)} %get-tuple-element.36), channel_id=1, source_target_pairs={{1,0},{2,1},{3,2},{5,4},{6,5},{7,6},{9,8},{10,9},{11,10},{13,12},{... | collective-permute-start | bytes 196616 | tf_op jit(solution)/shard_map/ppermute | solution.py:20
  230.5 6.4 %collective-permute-start.37 = (f32[2,8,8,128]{3,2,1,0:T(8,128)S(1)}, f32[2,8,8,128]{3,2,1,0:T(8,128)S(1)}, u32[]{:S(2)}, u32[]{:S(2)}) collective-permute-start(f32[2,8,8,128]{3,2,1,0:T(8,128)S(1)} %get-tuple-element.32), channel_id=1, source_target_pairs={{16,0},{17,1},{18,2},{19,3},{20,4},{21,5},{22,6},{23,7},{24,8},{25... | collective-permute-start | bytes 196616 | tf_op jit(solution)/shard_map/ppermute | solution.py:20
  245.2 7.0 %collective-permute-start.40 = (f32[12,12,2,128]{3,2,1,0:T(2,128)S(1)}, f32[12,12,2,128]{3,2,1,0:T(2,128)S(1)}, u32[]{:S(2)}, u32[]{:S(2)}) collective-permute-start(f32[12,12,2,128]{3,2,1,0:T(2,128)S(1)} %get-tuple-element.24), channel_id=1, source_target_pairs={{0,1},{1,2},{2,3},{4,5},{5,6},{6,7},{8,9},{9,10},{10,11},{12,13},{... | collective-permute-start | bytes 442376 | tf_op jit(solution)/shard_map/ppermute | solution.py:19
  247.1 7.0 %collective-permute-start.41 = (f32[12,12,2,128]{3,2,1,0:T(2,128)S(1)}, f32[12,12,2,128]{3,2,1,0:T(2,128)S(1)}, u32[]{:S(2)}, u32[]{:S(2)}) collective-permute-start(f32[12,12,2,128]{3,2,1,0:T(2,128)S(1)} %get-tuple-element.23), channel_id=1, source_target_pairs={{1,0},{2,1},{3,2},{5,4},{6,5},{7,6},{9,8},{10,9},{11,10},{13,12},{... | collective-permute-start | bytes 442376 | tf_op jit(solution)/shard_map/ppermute | solution.py:20
  258.8 8.3 %collective-permute-start.42 = (f32[2,16,16,128]{3,2,1,0:T(8,128)S(1)}, f32[2,16,16,128]{3,2,1,0:T(8,128)S(1)}, u32[]{:S(2)}, u32[]{:S(2)}) collective-permute-start(f32[2,16,16,128]{3,2,1,0:T(8,128)S(1)} %get-tuple-element.20), channel_id=1, source_target_pairs={{0,16},{1,17},{2,18},{3,19},{4,20},{5,21},{6,22},{7,23},{8,24},{9,... | collective-permute-start | bytes 786440 | tf_op jit(solution)/shard_map/ppermute | solution.py:19
  260.1 8.4 %collective-permute-start.43 = (f32[2,16,16,128]{3,2,1,0:T(8,128)S(1)}, f32[2,16,16,128]{3,2,1,0:T(8,128)S(1)}, u32[]{:S(2)}, u32[]{:S(2)}) collective-permute-start(f32[2,16,16,128]{3,2,1,0:T(8,128)S(1)} %get-tuple-element.21), channel_id=1, source_target_pairs={{16,0},{17,1},{18,2},{19,3},{20,4},{21,5},{22,6},{23,7},{24,8},{25... | collective-permute-start | bytes 786440 | tf_op jit(solution)/shard_map/ppermute | solution.py:20
  269.2 8.4 %collective-permute-start.44 = (f32[20,2,16,128]{3,2,1,0:T(8,128)S(1)}, f32[20,2,16,128]{3,2,1,0:T(8,128)S(1)}, u32[]{:S(2)}, u32[]{:S(2)}) collective-permute-start(f32[20,2,16,128]{3,2,1,0:T(8,128)S(1)} %get-tuple-element.16), channel_id=1, source_target_pairs={{0,4},{4,8},{8,12},{1,5},{5,9},{9,13},{2,6},{6,10},{10,14},{3,7},{... | collective-permute-start | bytes 983048 | tf_op jit(solution)/shard_map/ppermute | solution.py:19
  271.2 8.2 %collective-permute-start.45 = (f32[20,2,16,128]{3,2,1,0:T(8,128)S(1)}, f32[20,2,16,128]{3,2,1,0:T(8,128)S(1)}, u32[]{:S(2)}, u32[]{:S(2)}) collective-permute-start(f32[20,2,16,128]{3,2,1,0:T(8,128)S(1)} %get-tuple-element.17), channel_id=1, source_target_pairs={{4,0},{8,4},{12,8},{5,1},{9,5},{13,9},{6,2},{10,6},{14,10},{7,3},{... | collective-permute-start | bytes 983048 | tf_op jit(solution)/shard_map/ppermute | solution.py:20
  281.3 10.2 %collective-permute-start.46 = (f32[20,20,2,128]{3,2,1,0:T(2,128)}, f32[20,20,2,128]{3,2,1,0:T(2,128)}, u32[]{:S(2)}, u32[]{:S(2)}) collective-permute-start(f32[20,20,2,128]{3,2,1,0:T(2,128)} %get-tuple-element.13), channel_id=1, source_target_pairs={{0,1},{1,2},{2,3},{4,5},{5,6},{6,7},{8,9},{9,10},{10,11},{12,13},{... | collective-permute-start | bytes 1228808 | tf_op jit(solution)/shard_map/ppermute | solution.py:19
  283.2 10.4 %collective-permute-start.47 = (f32[20,20,2,128]{3,2,1,0:T(2,128)}, f32[20,20,2,128]{3,2,1,0:T(2,128)}, u32[]{:S(2)}, u32[]{:S(2)}) collective-permute-start(f32[20,20,2,128]{3,2,1,0:T(2,128)} %get-tuple-element.12), channel_id=1, source_target_pairs={{1,0},{2,1},{3,2},{5,4},{6,5},{7,6},{9,8},{10,9},{11,10},{13,12},{... | collective-permute-start | bytes 1228808 | tf_op jit(solution)/shard_map/ppermute | solution.py:20
  (43 other events, 433.5 us)
